TPU v7x, 32 devices: a whole 2x2x4 slice. The times are simulated.
32 devices in a mesh: grp: 4 (over y, x), dev: 8 (over z, core).
Axes of the slice: x: 2, y: 2, z: 4, core: 2. Of those that a mesh axis runs over, the one named last changes fastest.
Arguments:
- obs_coord: float32 [3, 131072], P(None, ('grp', 'dev')), may hold values from -1 to 1
- obs_resid: float32 [131072], P(('grp', 'dev')), may hold values from -6 to 6
- obs_weight: float32 [131072], P(('grp', 'dev')), may hold values from 0.5 to 2
- obs_dest: int32 [131072], P(('grp', 'dev')), may hold values from 0 to 7, as said below
- obs_send_slot: int32 [131072], P(('grp', 'dev')), may hold values from 0 to 1023, as said below
- obs_elem: int32 [131072], P(('grp', 'dev')), may hold values from 0 to 255, as said below
- obs_slot: int32 [131072], P(('grp', 'dev')), may hold values from 0 to 31, as said below
Outputs:
- nodal: float32 [16, 64, 8, 512], P('grp', 'dev')
- total_cost: float32 [], replicated
Inputs may be any that keep to these rules, and one draw needn't show every extreme that they name: `obs_dest`: from the rows of one device, at most 1024 observations go to any one destination; in every group one destination receives exactly 1024 from every device of the group. `obs_send_slot`: distinct among the rows of one device with the same obs_dest. `obs_elem`: together with obs_slot distinct among all observations of a group with the same obs_dest. `obs_slot`: on every destination some element uses all 32 slots.
All inputs are finite; a program needn't handle non-finite values.
Results may differ from a plain program's by a relative error of at most 0.00017.
Values sent between devices are 32-bit elements; how exact they have to be, the bound alone decides.
A program may use at most 64 MiB of HBM per device.

v0:
```python
import math

import jax
import jax.numpy as jnp
from jax import lax
from jax.sharding import PartitionSpec as P

EX = 4
EY = 8
EZ = 8
ELEM_DEV = 256
SLOTS = 32


def with_halo(block, sides, width):
    for axis, dim in sides:
        count = lax.axis_size(axis)
        forward = [(i, i + 1) for i in range(count - 1)]
        backward = [(target, source) for source, target in forward]
        low = lax.ppermute(
            lax.slice_in_dim(block, block.shape[dim] - width, None, axis=dim), axis, forward
        )
        high = lax.ppermute(lax.slice_in_dim(block, 0, width, axis=dim), axis, backward)
        block = jnp.concatenate([low, block, high], axis=dim)
    return block


def basis_values(position):
    anchors = [-math.cos(math.pi * k / 7) for k in range(8)]
    basis = []
    for node_i in range(8):
        factor = jnp.ones_like(position)
        for node_m in range(8):
            if node_m != node_i:
                factor = factor * (
                    (position - anchors[node_m]) / (anchors[node_i] - anchors[node_m])
                )
        basis.append(factor)
    return jnp.stack(basis)


def contract(first_w, second_w, third_w):
    outer = (first_w[:, None, :] * second_w[None, :, :]).reshape(64, ELEM_DEV, SLOTS)
    third = third_w.reshape(8, ELEM_DEV, SLOTS)
    mixed = jnp.einsum("aes,kes->eak", outer, third, precision=lax.Precision.HIGHEST)
    return mixed.reshape(ELEM_DEV, 512)


def combine(field, elem_dim, node_dim, from_low, from_high):
    count = field.shape[elem_dim]
    low_plane = lax.slice_in_dim(field, 0, 1, axis=node_dim)
    high_plane = lax.slice_in_dim(field, 7, 8, axis=node_dim)
    after = jnp.concatenate(
        [lax.slice_in_dim(low_plane, 1, count, axis=elem_dim), from_high], axis=elem_dim
    )
    before = jnp.concatenate(
        [from_low, lax.slice_in_dim(high_plane, 0, count - 1, axis=elem_dim)], axis=elem_dim
    )
    middle = lax.slice_in_dim(field, 1, 7, axis=node_dim)
    return jnp.concatenate([low_plane + before, middle, high_plane + after], axis=node_dim)


def boundary(field, elem_dim, node_dim):
    count = field.shape[elem_dim]
    low_plane = lax.slice_in_dim(field, 0, 1, axis=node_dim)
    high_plane = lax.slice_in_dim(field, 7, 8, axis=node_dim)
    return jnp.concatenate(
        [
            lax.slice_in_dim(low_plane, 0, 1, axis=elem_dim),
            lax.slice_in_dim(high_plane, count - 1, count, axis=elem_dim),
        ],
        axis=elem_dim,
    )


def on_device(obs_coord, obs_resid, obs_weight, obs_dest, obs_send_slot, obs_elem, obs_slot):
    peer_count = lax.axis_size("dev")
    row_count = obs_resid.shape[0]
    capacity = 2 * row_count // peer_count
    cell_count = ELEM_DEV * SLOTS
    forcing = obs_weight * obs_resid
    total_cost = lax.psum(0.5 * jnp.sum(forcing * obs_resid), ("grp", "dev"))
    payload = jnp.concatenate([obs_coord, forcing[None, :]], axis=0)
    channels = payload.shape[0]
    target = obs_dest * capacity + obs_send_slot
    cell_ids = obs_elem * SLOTS + obs_slot
    send_values = (
        jnp.zeros((channels, peer_count * capacity), payload.dtype).at[:, target].set(payload)
    )
    send_cells = jnp.full((peer_count * capacity,), cell_count, jnp.int32).at[target].set(cell_ids)
    send_values = send_values.reshape(channels, peer_count, capacity)
    send_cells = send_cells.reshape(1, peer_count, capacity)
    got_values, got_cells = (
        lax.all_to_all(send_values, "dev", split_axis=1, concat_axis=1, tiled=True),
        lax.all_to_all(send_cells, "dev", split_axis=1, concat_axis=1, tiled=True),
    )
    packed = jnp.zeros((channels, cell_count + 1), payload.dtype)
    packed = packed.at[:, got_cells.reshape(-1)].set(got_values.reshape(channels, -1))[
        :, :cell_count
    ]
    first_w = basis_values(packed[0]) * packed[3]
    second_w = basis_values(packed[1])
    third_w = basis_values(packed[2])
    field = contract(first_w, second_w, third_w).reshape(EX, EY, EZ, 8, 8, 8)
    padded = with_halo(boundary(field, 0, 3), (("grp", 0),), 1)
    field = combine(field, 0, 3, padded[0:1], padded[3:4])
    padded = with_halo(boundary(field, 1, 4), (("dev", 1),), 1)
    field = combine(field, 1, 4, padded[:, 0:1], padded[:, 3:4])
    empty = jnp.zeros_like(lax.slice_in_dim(lax.slice_in_dim(field, 0, 1, axis=5), 0, 1, axis=2))
    field = combine(field, 2, 5, empty, empty)
    return (field.reshape(EX, EY, EZ, 512), total_cost)


def solution(mesh):
    placed = (
        P(None, ("grp", "dev")),
        P(("grp", "dev")),
        P(("grp", "dev")),
        P(("grp", "dev")),
        P(("grp", "dev")),
        P(("grp", "dev")),
        P(("grp", "dev")),
    )
    return jax.shard_map(
        on_device,
        mesh=mesh,
        in_specs=placed,
        out_specs=(P("grp", "dev", None, None), P()),
        check_vma=False,
    )
```

profile of v0, /device:TPU:0, one launch (start us, length us, event | category | flops | bytes accessed | tf_op | source)
XLA Modules:
  0.0 223.1 jit_solution(2030563538721729877)
XLA Ops:
  0.6 0.8 compare_select_fusion.1
  1.4 16.1 %scatter_custom_fusion = s32[8192]{0:T(1024)} fusion(s32[4096]{0:T(1024)S(1)} %get-tuple-element.54, s32[4096]{0:T(1024)S(1)} %get-tuple-element.55, s32[]{:T(128)} %constant.245.clone.1), kind=kCustom, calls=%fused_computation.88 | custom fusion | bytes 32772 | tf_op jit(solution)/shard_map/scatter | solution.py:90
  17.5 6.4 %all-to-all-start = ((s32[1,8,1024]{2,0,1:T(1,128)}), s32[1,8,1024]{2,0,1:T(1,128)S(1)}, u32[]{:S(2)}, u32[]{:S(2)}) async-start(s32[1,8,1024]{2,0,1:T(1,128)} %bitcast), calls=%async_computation | async-start | bytes 65536 | tf_op jit(solution)/shard_map/all_to_all | solution.py:95
  23.8 1.3 multiply_reduce_fusion.8
  25.8 0.9 maximum_bitcast_fusion
  26.7 40.8 %psum.7 = f32[]{:T(128)} all-reduce(f32[]{:T(128)S(6)} %mul_shard_map.3), channel_id=1, replica_groups=mesh['grp'=4,'dev'=8] {'grp','dev'}, use_global_device_ids=true, to_apply=%region_4.0 | all-reduce | flops 1 | bytes 8 | tf_op jit(solution)/shard_map/psum | solution.py:82
  67.5 0.6 copy.404
  68.2 12.8 %scatter_custom_fusion.1 = f32[4,8192]{0,1:T(8,128)} fusion(s32[4096]{0:T(1024)S(1)} %get-tuple-element.54, f32[4096,4]{1,0:T(8,128)S(1)} %copy.404, f32[]{:T(128)} %constant.244.clone.1), kind=kCustom, calls=%fused_computation.11 | custom fusion | bytes 131076 | tf_op jit(solution)/shard_map/scatter | solution.py:88
  80.9 3.5 %copy.405 = f32[4,8,1024]{2,0,1:T(4,128)} copy(f32[4,8,1024]{0,2,1:T(8,128)} %bitcast.26) | data formatting | bytes 262144 | tf_op jit(solution)/shard_map/reshape | solution.py:91
  84.4 3.6 %all-to-all-start.1 = ((f32[4,8,1024]{2,0,1:T(4,128)}), f32[4,8,1024]{2,0,1:T(4,128)S(1)}, u32[]{:S(2)}, u32[]{:S(2)}) async-start(f32[4,8,1024]{2,0,1:T(4,128)} %copy.405), calls=%async_computation.1 | async-start | bytes 262144 | tf_op jit(solution)/shard_map/all_to_all | solution.py:94
  88.0 6.7 %all-to-all-done.1 = f32[4,8,1024]{2,0,1:T(4,128)S(1)} async-done(((f32[4,8,1024]{2,0,1:T(4,128)}), f32[4,8,1024]{2,0,1:T(4,128)S(1)}, u32[]{:S(2)}, u32[]{:S(2)}) %all-to-all-start.1) | async-done | bytes 131104 | tf_op jit(solution)/shard_map/all_to_all | solution.py:94
  94.7 2.6 %copy.406 = f32[8192,4]{1,0:T(8,128)} copy(f32[8192,4]{0,1:T(4,128)S(1)} %bitcast.35) | data formatting | bytes 262144 | tf_op jit(solution)/shard_map/reshape | solution.py:98
  97.3 23.0 %scatter_custom_fusion.2 = f32[4,8193]{0,1:T(8,128)} fusion(s32[8192]{0:T(1024)S(1)} %bitcast.38, f32[8192,4]{1,0:T(8,128)} %copy.406, f32[]{:T(128)} %constant.244.clone.1), kind=kCustom, calls=%fused_computation.9 | custom fusion | bytes 131600 | tf_op jit(solution)/shard_map/scatter | solution.py:98
  120.4 14.8 %slice_reduce_fusion = (f32[8192]{0:T(1024)S(1)}, f32[1,8192]{0,1:T(8,128)}, f32[1,8192]{0,1:T(8,128)}, f32[1,8192]{0,1:T(8,128)}) fusion(f32[4,8193]{0,1:T(8,128)} %scatter_custom_fusion.2), kind=kLoop, calls=%fused_computation.8 | loop fusion | bytes 262144 | tf_op jit(solution)/shard_map/slice | solution.py:101
  135.2 2.8 %copy.422 = f32[1,8192]{1,0:T(1,128)S(1)} copy(f32[1,8192]{0,1:T(8,128)} %get-tuple-element.35) | data formatting | bytes 65536
  138.0 2.8 %copy.421 = f32[1,8192]{1,0:T(1,128)S(1)} copy(f32[1,8192]{0,1:T(8,128)} %get-tuple-element.36) | data formatting | bytes 65536
  140.8 2.8 %copy.423 = f32[1,8192]{1,0:T(1,128)S(1)} copy(f32[1,8192]{0,1:T(8,128)} %get-tuple-element.37) | data formatting | bytes 65536
  143.7 1.9 multiply_reduce_fusion
  145.7 0.1 stack.57
  146.2 0.8 stack.24
  147.0 1.0 multiply_multiply_fusion.8
  148.0 1.0 multiply_multiply_fusion
  148.9 0.4 stack.22
  149.4 0.4 stack.23
  149.8 0.1 broadcast_multiply_fusion
  149.9 4.8 %mul.732 = f32[64,256,32]{2,1,0:T(8,128)} reshape(f32[8,8,8192]{2,1,0:T(8,128)S(1)} %broadcast_multiply_fusion) | data formatting | bytes 4194304 | tf_op jit(solution)/shard_map/mul | solution.py:43
  154.7 1.6 stack.59
  156.4 20.7 %fusion = f32[256,64,8]{1,2,0:T(8,128)S(1)} fusion(f32[8,256,32]{2,0,1:T(8,128)S(1)} %stack.59, f32[64,256,32]{2,1,0:T(8,128)} %mul.732), kind=kOutput, calls=%fused_computation.6 | convolution fusion | flops 50331648 | bytes 2883584 | tf_op jit(solution)/shard_map/aes,kes->eak/dot_general | solution.py:45
  177.0 0.5 copy.419
  177.5 6.2 %reshape_reshape.3 = f32[4,8,8,8,8,8]{2,1,0,5,4,3:T(8,128)} reshape(f32[256,64,8]{0,2,1:T(8,128)S(1)} %copy.419) | data formatting | bytes 1048576 | tf_op jit(solution)/shard_map/reshape;reshape | solution.py:104
  183.7 1.1 fusion.14
  184.7 4.2 %collective-permute-start = (f32[1,8,8,1,8,8]{2,1,0,5,4,3:T(8,128)S(1)}, f32[1,8,8,1,8,8]{2,1,0,5,4,3:T(8,128)S(1)}, u32[]{:S(2)}, u32[]{:S(2)}) collective-permute-start(f32[1,8,8,1,8,8]{2,1,0,5,4,3:T(8,128)S(1)} %get-tuple-element.30), channel_id=1, source_target_pairs={{0,8},{8,16},{16,24},{1,9},{9,17},{17,25},{2,10},{10,18},{18,26},{... | collective-permute-start | bytes 49160 | tf_op jit(solution)/shard_map/ppermute | solution.py:20
  188.9 1.3 collective-permute-start.1
  190.2 1.5 fusion.15
  191.7 3.5 %slice.118 = f32[4,8,8,6,8,8]{2,1,0,5,4,3:T(8,128)S(1)} slice(f32[4,8,8,8,8,8]{2,1,0,5,4,3:T(8,128)} %reshape_reshape.3), slice={[0:4], [0:8], [0:8], [1:7], [0:8], [0:8]} | slice | bytes 786432 | tf_op jit(solution)/shard_map/slice | solution.py:59
  195.3 6.6 %collective-permute-done.1 = f32[1,8,8,1,8,8]{2,1,0,5,4,3:T(8,128)S(1)} collective-permute-done((f32[1,8,8,1,8,8]{2,1,0,5,4,3:T(8,128)S(1)}, f32[1,8,8,1,8,8]{2,1,0,5,4,3:T(8,128)S(1)}, u32[]{:S(2)}, u32[]{:S(2)}) %collective-permute-start.1) | collective-permute-done | bytes 16416 | tf_op jit(solution)/shard_map/ppermute | solution.py:23
  201.9 1.9 slice_add_fusion.1
  203.8 0.3 pad_maximum_fusion.8
  204.1 1.3 collective-permute-start.2
  205.4 1.3 collective-permute-start.3
  206.7 1.9 pad_maximum_fusion
  208.6 1.2 slice.122
  209.9 0.5 fusion.11
  210.5 0.6 fusion.7
  211.1 1.6 pad_maximum_fusion.1
  212.7 0.8 slice.123
  213.5 3.7 %pad_maximum_fusion.2 = f32[4,8,8,8,8,8]{2,1,0,5,4,3:T(8,128)} fusion(f32[4,8,8,8,8,1]{2,1,0,5,4,3:T(8,128)S(1)} %get-tuple-element.23, f32[4,8,8,8,8,6]{2,1,0,5,4,3:T(8,128)S(1)} %slice.123, f32[4,8,8,8,8,1]{2,1,0,5,4,3:T(8,128)S(1)} %get-tuple-element.22), kind=kLoop, calls=%fused_computation.5 | loop fusion | flops 262144 | bytes 1048576 | tf_op jit(solution)/shard_map/concatenate | solution.py:60
  217.3 5.9 %copy.420 = f32[4,8,8,512]{3,2,1,0:T(8,128)} copy(f32[4,8,8,512]{2,1,0,3:T(8,128)} %bitcast.25) | data formatting | bytes 1048576
  (14 shorter events, 0.6 us)
Async XLA Ops:
  17.5 66.9 %all-to-all-start = ((s32[1,8,1024]{2,0,1:T(1,128)}), s32[1,8,1024]{2,0,1:T(1,128)S(1)}, u32[]{:S(2)}, u32[]{:S(2)}) async-start(s32[1,8,1024]{2,0,1:T(1,128)} %bitcast), calls=%async_computation | async-start | bytes 65536 | tf_op jit(solution)/shard_map/all_to_all | solution.py:95
  84.4 10.3 %all-to-all-start.1 = ((f32[4,8,1024]{2,0,1:T(4,128)}), f32[4,8,1024]{2,0,1:T(4,128)S(1)}, u32[]{:S(2)}, u32[]{:S(2)}) async-start(f32[4,8,1024]{2,0,1:T(4,128)} %copy.405), calls=%async_computation.1 | async-start | bytes 262144 | tf_op jit(solution)/shard_map/all_to_all | solution.py:94
  149.9 4.8 %copy-start = (f32[1,256,32]{2,1,0:T(8,128)S(1)}, f32[1,256,32]{2,1,0:T(8,128)}, u32[]{:S(2)}) copy-start(f32[1,256,32]{2,1,0:T(8,128)} %stack.24) | copy-start | bytes 98308
  184.7 10.5 %collective-permute-start = (f32[1,8,8,1,8,8]{2,1,0,5,4,3:T(8,128)S(1)}, f32[1,8,8,1,8,8]{2,1,0,5,4,3:T(8,128)S(1)}, u32[]{:S(2)}, u32[]{:S(2)}) collective-permute-start(f32[1,8,8,1,8,8]{2,1,0,5,4,3:T(8,128)S(1)} %get-tuple-element.30), channel_id=1, source_target_pairs={{0,8},{8,16},{16,24},{1,9},{9,17},{17,25},{2,10},{10,18},{18,26},{... | collective-permute-start | bytes 49160 | tf_op jit(solution)/shard_map/ppermute | solution.py:20
  188.9 13.0 %collective-permute-start.1 = (f32[1,8,8,1,8,8]{2,1,0,5,4,3:T(8,128)S(1)}, f32[1,8,8,1,8,8]{2,1,0,5,4,3:T(8,128)S(1)}, u32[]{:S(2)}, u32[]{:S(2)}) collective-permute-start(f32[1,8,8,1,8,8]{2,1,0,5,4,3:T(8,128)S(1)} %get-tuple-element.31), channel_id=1, source_target_pairs={{8,0},{16,8},{24,16},{9,1},{17,9},{25,17},{10,2},{18,10},{26,18},{... | collective-permute-start | bytes 49160 | tf_op jit(solution)/shard_map/ppermute | solution.py:23
  204.1 5.7 %collective-permute-start.2 = (f32[4,1,8,8,1,8]{2,1,0,5,4,3:T(1,128)S(1)}, f32[4,1,8,8,1,8]{2,1,0,5,4,3:T(1,128)S(1)}, u32[]{:S(2)}, u32[]{:S(2)}) collective-permute-start(f32[4,1,8,8,1,8]{2,1,0,5,4,3:T(1,128)S(1)} %get-tuple-element.26), channel_id=1, source_target_pairs={{0,1},{1,2},{2,3},{3,4},{4,5},{5,6},{6,7},{8,9},{9,10},{10,11},{11... | collective-permute-start | bytes 24584 | tf_op jit(solution)/shard_map/ppermute | solution.py:20
  205.4 4.5 %collective-permute-start.3 = (f32[4,1,8,8,1,8]{2,1,0,5,4,3:T(1,128)S(1)}, f32[4,1,8,8,1,8]{2,1,0,5,4,3:T(1,128)S(1)}, u32[]{:S(2)}, u32[]{:S(2)}) collective-permute-start(f32[4,1,8,8,1,8]{2,1,0,5,4,3:T(1,128)S(1)} %get-tuple-element.27), channel_id=1, source_target_pairs={{1,0},{2,1},{3,2},{4,3},{5,4},{6,5},{7,6},{9,8},{10,9},{11,10},{12... | collective-permute-start | bytes 24584 | tf_op jit(solution)/shard_map/ppermute | solution.py:23
where the time goes:
time: 227 us; the launch traced here: 223 us
  local copies, waits for them, and re-layouts  111 us (49%)
  blocking collectives  40.8 us (18%)
  matrix products  20.7 us (9%)
  starting transfers between devices  18 us (8%)
  other arithmetic  17.6 us (8%)
  waiting for transfers between devices  13.4 us (6%)
    psum x1, blocking collectives, on_device(): total_cost = lax.psum(0.5 * jnp.sum(forcing * obs_resid), ('grp', 'dev'))  40.8 us
    scatter x1, local copies, waits for them, and re-layouts, on_device(): packed.at[:, got_cells.reshape(-1)].set(got_values.reshape(channels, -1))  23 us
    dot_general x1, matrix products, contract(): jnp.einsum('aes,kes->eak', outer, third, precision=lax.Precision.HIGHEST)  20.7 us
    scatter x1, local copies, waits for them, and re-layouts, on_device(): jnp.full((peer_count * capacity,), cell_count, jnp.int32).at[target]  16.1 us
    slice x1, local copies, waits for them, and re-layouts, on_device(): first_w = basis_values(packed[0]) * packed[3]  14.8 us
    unnamed x6, local copies, waits for them, and re-layouts  14.4 us
    scatter x1, local copies, waits for them, and re-layouts, on_device(): jnp.zeros((channels, peer_count * capacity), payload.dtype).at[:, target]  12.8 us
    concatenate x3, other arithmetic, combine(): jnp.concatenate([low_plane + before, middle, high_plane + after], axis=no...  7.23 us
  transfers between devices with their start and end apart: 6, of which 3 were waited for; matrix products, arithmetic and copies ran while one was open for 12% of the time, Pallas kernels for 0%

commit v1 on v0

v1 whole, which is shorter than its diff:
```python
import functools
import math

import jax
import jax.numpy as jnp
from jax import lax
from jax.experimental import pallas as pl
from jax.experimental.pallas import tpu as pltpu
from jax.sharding import PartitionSpec as P

EX = 4
EY = 8
EZ = 8
ELEM_DEV = 256
LANES = 128
CHUNK = 1024
MESH = pl.DeviceIdType.MESH
F32 = jnp.float32
BF16 = jnp.bfloat16

ANCHORS = [-math.cos(math.pi * k / 7) for k in range(8)]
COEFS = [
    1.0 / math.prod(ANCHORS[a] - ANCHORS[m] for m in range(8) if m != a) for a in range(8)
]


def basis_values(t):
    factors = [t - p for p in ANCHORS]
    prefix = [None] * 8
    suffix = [None] * 8
    for k in range(1, 8):
        prefix[k] = factors[k - 1] if k == 1 else prefix[k - 1] * factors[k - 1]
    for k in range(6, -1, -1):
        suffix[k] = factors[k + 1] if k == 6 else suffix[k + 1] * factors[k + 1]
    basis = []
    for a in range(8):
        if a == 0:
            product = suffix[0]
        elif a == 7:
            product = prefix[7]
        else:
            product = prefix[a] * suffix[a]
        basis.append(product * COEFS[a])
    return basis


def dot_nt(left, right):
    return lax.dot_general(left, right, (((1,), (1,)), ((), ())), preferred_element_type=F32)


def split3(value):
    first = value.astype(BF16).astype(F32)
    rest = value - first
    second = rest.astype(BF16).astype(F32)
    return first, second, rest - second


def kernel(
    dev_count, grp_count, capacity,
    coord, resid, weight, dest, slot, elem,
    out, cost,
    acc, send, recv, cost_send, cost_recv, group_send, group_recv,
    third, outer, p_high, p_low, onehot, raw, a_send, a_recv, b_send, b_recv,
    send_sem, recv_sem, cost_send_sem, cost_recv_sem, group_send_sem, group_recv_sem,
    face_send_sem, face_recv_sem,
):
    g = lax.axis_index("grp")
    d = lax.axis_index("dev")
    row_count = resid.shape[1]
    row_total = 2 * row_count // LANES
    per_dest = capacity // LANES
    per_chunk = 8 // per_dest

    barrier = pltpu.get_barrier_semaphore()
    for j in range(1, dev_count):
        pl.semaphore_signal(
            barrier, inc=1, device_id=(g, lax.rem(d + j, dev_count)), device_id_type=MESH
        )
    for j in range(1, grp_count):
        pl.semaphore_signal(
            barrier, inc=1, device_id=(lax.rem(g + j, grp_count), d), device_id_type=MESH
        )

    acc[...] = jnp.zeros_like(acc)

    def pack(k, total):
        columns = pl.ds(pl.multiple_of(k * CHUNK, CHUNK), CHUNK)
        target = dest[:, columns] * capacity + slot[:, columns]
        high = jnp.broadcast_to(target // LANES, (row_total, CHUNK))
        low = jnp.broadcast_to(target % LANES, (LANES, CHUNK))
        row_hot = jnp.where(
            lax.broadcasted_iota(jnp.int32, (row_total, CHUNK), 0) == high, 1.0, 0.0
        ).astype(BF16)
        lane_hot = jnp.where(
            lax.broadcasted_iota(jnp.int32, (LANES, CHUNK), 0) == low, 1.0, 0.0
        ).astype(BF16)
        residual = resid[:, columns]
        forcing = weight[:, columns] * residual
        values = [coord[c : c + 1, columns] for c in range(3)] + [forcing]
        terms = [split3(value) for value in values]

        def spread(row):
            tile = jnp.broadcast_to(row, (16, CHUNK)).astype(BF16)
            return [row_hot[16 * i : 16 * i + 16] * tile for i in range(row_total // 16)]

        for t in range(3):
            pieces = []
            for channel in range(4):
                pieces += spread(terms[channel][t])
            if t == 0:
                pieces += spread(elem[:, columns].astype(F32))
            left = jnp.concatenate(pieces, axis=0)
            acc[0 : left.shape[0], :] += dot_nt(left, lane_hot)
        return total + forcing * residual

    total = lax.fori_loop(0, row_count // CHUNK, pack, jnp.zeros((1, CHUNK), F32))
    part = jnp.broadcast_to(0.5 * jnp.sum(total, axis=1, keepdims=True), (1, LANES))
    cost_send[...] = part
    for p in range(dev_count):
        for c in range(5):
            start = c * row_total + p * per_dest
            send[p, c * per_dest : (c + 1) * per_dest, :] = acc[start : start + per_dest, :]

    pl.semaphore_wait(barrier, dev_count - 1 + grp_count - 1)

    def data_copy(j):
        peer = lax.rem(d + j, dev_count)
        return pltpu.make_async_remote_copy(
            src_ref=send.at[peer], dst_ref=recv.at[j],
            send_sem=send_sem.at[j], recv_sem=recv_sem.at[j],
            device_id=(g, peer), device_id_type=MESH,
        )

    def cost_copy(j):
        return pltpu.make_async_remote_copy(
            src_ref=cost_send, dst_ref=cost_recv.at[j],
            send_sem=cost_send_sem.at[j], recv_sem=cost_recv_sem.at[j],
            device_id=(g, lax.rem(d + j, dev_count)), device_id_type=MESH,
        )

    def group_copy(j):
        return pltpu.make_async_remote_copy(
            src_ref=group_send, dst_ref=group_recv.at[j],
            send_sem=group_send_sem.at[j], recv_sem=group_recv_sem.at[j],
            device_id=(lax.rem(g + j, grp_count), d), device_id_type=MESH,
        )

    for j in range(1, dev_count):
        data_copy(j).start()
    for j in range(1, dev_count):
        cost_copy(j).start()
    recv[0] = send[d]

    raw[...] = jnp.zeros_like(raw)

    def element_sums(k, carry):
        for i in range(per_chunk):
            @pl.when(k * per_chunk + i > 0)
            def _():
                data_copy(k * per_chunk + i).wait_recv()

        def channel(c):
            rows = [
                recv[k * per_chunk + i, c * per_dest : (c + 1) * per_dest, :]
                for i in range(per_chunk)
            ]
            return rows[0] if per_chunk == 1 else jnp.concatenate(rows, axis=0)

        first_w = basis_values(channel(0))
        second_w = basis_values(channel(1))
        third_w = basis_values(channel(2))
        forcing = channel(3)
        owner = channel(4).astype(jnp.int32)
        for a in range(8):
            weighted = first_w[a] * forcing
            third[a] = third_w[a]
            for b in range(8):
                outer[a * 8 + b] = weighted * second_w[b]
        ids = lax.broadcasted_iota(jnp.int32, (ELEM_DEV, LANES), 0)
        for h in range(8):
            lanes = slice(h * LANES, (h + 1) * LANES)
            product = (outer[:, h : h + 1, :] * third[:, h, :][None]).reshape(512, LANES)
            rounded = product.astype(BF16)
            p_high[:, lanes] = rounded
            p_low[:, lanes] = (product - rounded.astype(F32)).astype(BF16)
            onehot[:, lanes] = jnp.where(
                ids == jnp.broadcast_to(owner[h : h + 1, :], (ELEM_DEV, LANES)), 1.0, 0.0
            ).astype(BF16)
        raw[...] += dot_nt(p_high[...], onehot[...]) + dot_nt(p_low[...], onehot[...])
        return carry

    lax.fori_loop(0, dev_count // per_chunk, element_sums, 0)

    group_cost = cost_send[...]
    for j in range(1, dev_count):
        cost_copy(j).wait_recv()
        group_cost = group_cost + cost_recv[j]
    group_send[...] = group_cost
    for j in range(1, grp_count):
        group_copy(j).start()

    lane = lax.broadcasted_iota(jnp.int32, (1, LANES), 1)
    lower_half = lane < 64
    block = raw[448:512, 128:256]
    a_send[0] = jnp.where(lower_half, pltpu.roll(block[0:32], 64, 1), block[32:64])
    block = raw[0:64, 0:128]
    a_send[1] = jnp.where(lower_half, block[0:32], pltpu.roll(block[32:64], 64, 1))

    def face_copy(i):
        step = 1 if i % 2 == 0 else -1
        if i < 2:
            source, sink = a_send.at[i], a_recv.at[i]
            target = (lax.rem(g + step + grp_count, grp_count), d)
        else:
            source, sink = b_send.at[i - 2], b_recv.at[i - 2]
            target = (g, lax.rem(d + step + dev_count, dev_count))
        return pltpu.make_async_remote_copy(
            src_ref=source, dst_ref=sink,
            send_sem=face_send_sem.at[i], recv_sem=face_recv_sem.at[i],
            device_id=target, device_id_type=MESH,
        )

    def start_faces(first, position, count):
        @pl.when(position < count - 1)
        def _():
            face_copy(first).start()

        @pl.when(position > 0)
        def _():
            face_copy(first + 1).start()

    def finish_faces(first, position, count, sink):
        @pl.when(position > 0)
        def _():
            face_copy(first).wait_recv()

        @pl.when(position == 0)
        def _():
            sink[0] = jnp.zeros_like(sink[0])

        @pl.when(position < count - 1)
        def _():
            face_copy(first + 1).wait_recv()

        @pl.when(position == count - 1)
        def _():
            sink[1] = jnp.zeros_like(sink[1])

    start_faces(0, g, grp_count)
    finish_faces(0, g, grp_count, a_recv)
    low, high = raw[0:64, :], raw[448:512, :]
    from_low, from_high = a_recv[0], a_recv[1]
    from_low = jnp.concatenate([from_low, pltpu.roll(from_low, 64, 1)], axis=0)
    from_high = jnp.concatenate([pltpu.roll(from_high, 64, 1), from_high], axis=0)
    high_rolled = [pltpu.roll(high[:, :128], 64, 1), pltpu.roll(high[:, 128:], 64, 1)]
    low_rolled = [pltpu.roll(low[:, :128], 64, 1), pltpu.roll(low[:, 128:], 64, 1)]
    raw[0:64, 0:128] = low[:, :128] + jnp.where(lower_half, from_low, high_rolled[0])
    raw[0:64, 128:256] = low[:, 128:] + jnp.where(lower_half, high_rolled[0], high_rolled[1])
    raw[448:512, 0:128] = high[:, :128] + jnp.where(lower_half, low_rolled[0], low_rolled[1])
    raw[448:512, 128:256] = high[:, 128:] + jnp.where(lower_half, low_rolled[1], from_high)

    ey = (lane // 8) % 8
    for half in range(2):
        columns = slice(half * LANES, (half + 1) * LANES)
        up = raw[56:64, columns]
        up = pltpu.roll(up, 72, 1)
        down = raw[0:8, columns]
        for a in range(1, 8):
            up = jnp.where(
                ey == a, pltpu.roll(raw[a * 64 + 56 : a * 64 + 64, columns], (a * 8 + 72) % 128, 1), up
            )
            down = jnp.where(
                ey == a, pltpu.roll(raw[a * 64 : a * 64 + 8, columns], a * 8, 1), down
            )
        b_send[0, half] = up
        b_send[1, half] = down
    start_faces(2, d, dev_count)
    finish_faces(2, d, dev_count, b_recv)
    for half in range(2):
        columns = slice(half * LANES, (half + 1) * LANES)
        from_low, from_high = b_recv[0, half], b_recv[1, half]
        for a in range(8):
            low_rows = slice(a * 64, a * 64 + 8)
            high_rows = slice(a * 64 + 56, a * 64 + 64)
            low, high = raw[low_rows, columns], raw[high_rows, columns]
            got_low = pltpu.roll(from_low, (128 - a * 8) % 128, 1)
            got_high = pltpu.roll(from_high, (56 - a * 8) % 128, 1)
            raw[low_rows, columns] = low + jnp.where(ey == 0, got_low, pltpu.roll(high, 8, 1))
            raw[high_rows, columns] = high + jnp.where(ey == 7, got_high, pltpu.roll(low, 120, 1))

    ez = lax.broadcasted_iota(jnp.int32, (1, 8, LANES), 2) % 8
    c = lax.broadcasted_iota(jnp.int32, (1, 8, LANES), 1)
    takes_low = (c == 0) & (ez > 0)
    takes_high = (c == 7) & (ez < 7)
    for half in range(2):
        for part in range(4):
            rows = slice(part * 128, (part + 1) * 128)
            field = raw[rows, half * LANES : (half + 1) * LANES].reshape(16, 8, LANES)
            below = pltpu.roll(pltpu.roll(field, 1, 2), 1, 1)
            above = pltpu.roll(pltpu.roll(field, 127, 2), 7, 1)
            field = field + jnp.where(takes_low, below, jnp.where(takes_high, above, 0.0))
            out[half * LANES : (half + 1) * LANES, rows] = field.reshape(128, LANES).T

    all_cost = group_send[...]
    for j in range(1, grp_count):
        group_copy(j).wait_recv()
        all_cost = all_cost + group_recv[j]
    cost[...] = all_cost

    for j in range(1, dev_count):
        data_copy(j).wait_send()
        cost_copy(j).wait_send()
    for j in range(1, grp_count):
        group_copy(j).wait_send()
    for first, position, count in ((0, g, grp_count), (2, d, dev_count)):
        @pl.when(position < count - 1)
        def _():
            face_copy(first).wait_send()

        @pl.when(position > 0)
        def _():
            face_copy(first + 1).wait_send()


def on_device(obs_coord, obs_resid, obs_weight, obs_dest, obs_send_slot, obs_elem, obs_slot):
    dev_count = lax.axis_size("dev")
    grp_count = lax.axis_size("grp")
    row_count = obs_resid.shape[0]
    capacity = 2 * row_count // dev_count
    per_dest = capacity // LANES
    vmem = pl.BlockSpec(memory_space=pltpu.VMEM)
    dma = pltpu.SemaphoreType.DMA
    rows = [x.reshape(1, row_count) for x in (obs_resid, obs_weight, obs_dest, obs_send_slot, obs_elem)]
    field, cost = pl.pallas_call(
        functools.partial(kernel, dev_count, grp_count, capacity),
        out_shape=(
            jax.ShapeDtypeStruct((ELEM_DEV, 512), F32),
            jax.ShapeDtypeStruct((1, LANES), F32),
        ),
        in_specs=[vmem] * 6,
        out_specs=(vmem, vmem),
        scratch_shapes=[
            pltpu.VMEM((5 * 2 * row_count // LANES, LANES), F32),
            pltpu.VMEM((dev_count, 5 * per_dest, LANES), F32),
            pltpu.VMEM((dev_count, 5 * per_dest, LANES), F32),
            pltpu.VMEM((1, LANES), F32),
            pltpu.VMEM((dev_count, 1, LANES), F32),
            pltpu.VMEM((1, LANES), F32),
            pltpu.VMEM((grp_count, 1, LANES), F32),
            pltpu.VMEM((8, 8, LANES), F32),
            pltpu.VMEM((64, 8, LANES), F32),
            pltpu.VMEM((512, CHUNK), BF16),
            pltpu.VMEM((512, CHUNK), BF16),
            pltpu.VMEM((ELEM_DEV, CHUNK), BF16),
            pltpu.VMEM((512, ELEM_DEV), F32),
            pltpu.VMEM((2, 32, LANES), F32),
            pltpu.VMEM((2, 32, LANES), F32),
            pltpu.VMEM((2, 2, 8, LANES), F32),
            pltpu.VMEM((2, 2, 8, LANES), F32),
            dma((dev_count,)),
            dma((dev_count,)),
            dma((dev_count,)),
            dma((dev_count,)),
            dma((grp_count,)),
            dma((grp_count,)),
            dma((4,)),
            dma((4,)),
        ],
        compiler_params=pltpu.CompilerParams(collective_id=0, has_side_effects=True),
    )(obs_coord, *rows)
    return field.reshape(EX, EY, EZ, 512), cost[0, 0]


def solution(mesh):
    placed = (
        P(None, ("grp", "dev")),
        P(("grp", "dev")),
        P(("grp", "dev")),
        P(("grp", "dev")),
        P(("grp", "dev")),
        P(("grp", "dev")),
        P(("grp", "dev")),
    )
    return jax.shard_map(
        on_device,
        mesh=mesh,
        in_specs=placed,
        out_specs=(P("grp", "dev", None, None), P()),
        check_vma=False,
    )
```

time: 227 us -> 26.9 us (0.12)
  the two profiles are of different devices: /device:TPU:0 before, /device:TPU:1 now
where the time goes in v1:
time: 26.9 us; the launch traced here: 26.7 us
  Pallas kernels  23 us (86%)
  local copies, waits for them, and re-layouts  1.87 us (7%)
  between operations  1.81 us (7%)
    pallas_call x1, Pallas kernels, on_device(): pl.pallas_call(functools.partial(kernel, dev_count, grp_count, capacity),...  23 us
    unnamed x3, local copies, waits for them, and re-layouts  1.87 us

profile of v1, /device:TPU:1, one launch (start us, length us, event | category | flops | bytes accessed | tf_op | source)
XLA Modules:
  0.0 26.7 jit_solution(9444521515495283281)
XLA Ops:
  0.6 23.0 %shard_map.77 = (f32[256,512]{1,0:T(8,128)}, f32[1,128]{1,0:T(1,128)}) custom-call(f32[3,4096]{1,0:T(4,128)} %coord.1, f32[1,4096]{1,0:T(1,128)} %bitcast.9, f32[1,4096]{1,0:T(1,128)} %bitcast.10, s32[1,4096]{1,0:T(1,128)} %bitcast.11, s32[1,4096]{1,0:T(1,128)} %bitcast.12, s32[1,4096]{1,0:T(1,128)} %bitcast.13), custom_call_target="tpu_custom_call" | custom-call | tf_op jit(solution)/shard_map/pallas_call | solution.py:334
  23.6 0.0 copy-start
  23.6 1.9 %copy.10 = f32[4,8,8,512]{3,2,1,0:T(8,128)} copy(f32[4,8,8,512]{3,2,1,0:T(8,128)} %bitcast.8) | data formatting | bytes 1048576
  25.5 0.0 copy-done
Async XLA Ops:
  23.6 1.9 %copy-start = (f32[1,128]{1,0:T(1,128)S(1)}, f32[1,128]{1,0:T(1,128)}, u32[]{:S(2)}) copy-start(f32[1,128]{1,0:T(1,128)} %get-tuple-element.5) | copy-start | bytes 1540

commit v2 on v1

--- a/solution.py
+++ b/solution.py
@@ -57,12 +57,12 @@
 
 def kernel(
     dev_count, grp_count, capacity,
-    coord, resid, weight, dest, slot, elem,
+    coord_in, resid_in, weight_in, dest_in, slot_in, elem_in,
     out, cost,
-    acc, send, recv, cost_send, cost_recv, group_send, group_recv,
+    coord, resid, weight, dest, slot, elem, acc, send, recv, cost_send, cost_recv, group_send, group_recv,
     third, outer, p_high, p_low, onehot, raw, a_send, a_recv, b_send, b_recv,
     send_sem, recv_sem, cost_send_sem, cost_recv_sem, group_send_sem, group_recv_sem,
-    face_send_sem, face_recv_sem,
+    face_send_sem, face_recv_sem, edge_recv, edge_send_sem, edge_recv_sem, load_sem,
 ):
     g = lax.axis_index("grp")
     d = lax.axis_index("dev")
@@ -71,15 +71,39 @@
     per_dest = capacity // LANES
     per_chunk = 8 // per_dest
 
+    def peer_of(k):
+        peer, bit = 0, 1
+        while bit < dev_count:
+            peer = peer + lax.rem(d // bit + k // bit, 2) * bit
+            bit *= 2
+        return peer
+
+    def wrapped(step_g, step_d):
+        return (
+            lax.rem(g + step_g + grp_count, grp_count),
+            lax.rem(d + step_d + dev_count, dev_count),
+        )
+
     barrier = pltpu.get_barrier_semaphore()
-    for j in range(1, dev_count):
-        pl.semaphore_signal(
-            barrier, inc=1, device_id=(g, lax.rem(d + j, dev_count)), device_id_type=MESH
-        )
-    for j in range(1, grp_count):
-        pl.semaphore_signal(
-            barrier, inc=1, device_id=(lax.rem(g + j, grp_count), d), device_id_type=MESH
-        )
+    partners = [(g, peer_of(k)) for k in range(1, dev_count)]
+    partners += [wrapped(j, 0) for j in range(1, grp_count)]
+    partners += [wrapped(i, j) for i in (-1, 1) for j in (-1, 1)]
+    for partner in partners:
+        pl.semaphore_signal(barrier, inc=1, device_id=partner, device_id_type=MESH)
+
+    loads = [
+        pltpu.make_async_copy(source, sink, load_sem.at[i])
+        for i, (source, sink) in enumerate(
+            zip(
+                (dest_in, slot_in, resid_in, weight_in, coord_in, elem_in),
+                (dest, slot, resid, weight, coord, elem),
+            )
+        )
+    ]
+    for load in loads:
+        load.start()
+    for load in loads:
+        load.wait()
 
     acc[...] = jnp.zeros_like(acc)
 
@@ -121,10 +145,10 @@
             start = c * row_total + p * per_dest
             send[p, c * per_dest : (c + 1) * per_dest, :] = acc[start : start + per_dest, :]
 
-    pl.semaphore_wait(barrier, dev_count - 1 + grp_count - 1)
+    pl.semaphore_wait(barrier, len(partners))
 
     def data_copy(j):
-        peer = lax.rem(d + j, dev_count)
+        peer = peer_of(j)
         return pltpu.make_async_remote_copy(
             src_ref=send.at[peer], dst_ref=recv.at[j],
             send_sem=send_sem.at[j], recv_sem=recv_sem.at[j],
@@ -135,20 +159,20 @@
         return pltpu.make_async_remote_copy(
             src_ref=cost_send, dst_ref=cost_recv.at[j],
             send_sem=cost_send_sem.at[j], recv_sem=cost_recv_sem.at[j],
-            device_id=(g, lax.rem(d + j, dev_count)), device_id_type=MESH,
+            device_id=(g, peer_of(j)), device_id_type=MESH,
         )
 
     def group_copy(j):
         return pltpu.make_async_remote_copy(
             src_ref=group_send, dst_ref=group_recv.at[j],
             send_sem=group_send_sem.at[j], recv_sem=group_recv_sem.at[j],
-            device_id=(lax.rem(g + j, grp_count), d), device_id_type=MESH,
-        )
-
+            device_id=wrapped(j, 0), device_id_type=MESH,
+        )
+
+    for j in range(1, dev_count):
+        cost_copy(j).start()
     for j in range(1, dev_count):
         data_copy(j).start()
-    for j in range(1, dev_count):
-        cost_copy(j).start()
     recv[0] = send[d]
 
     raw[...] = jnp.zeros_like(raw)
@@ -189,7 +213,9 @@
         raw[...] += dot_nt(p_high[...], onehot[...]) + dot_nt(p_low[...], onehot[...])
         return carry
 
-    lax.fori_loop(0, dev_count // per_chunk, element_sums, 0)
+    chunk_count = dev_count // per_chunk
+    middle = chunk_count // 2
+    lax.fori_loop(0, middle, element_sums, 0)
 
     group_cost = cost_send[...]
     for j in range(1, dev_count):
@@ -199,55 +225,68 @@
     for j in range(1, grp_count):
         group_copy(j).start()
 
+    lax.fori_loop(middle, chunk_count, element_sums, 0)
+
     lane = lax.broadcasted_iota(jnp.int32, (1, LANES), 1)
     lower_half = lane < 64
+    node = (lane // 8) % 8
     block = raw[448:512, 128:256]
     a_send[0] = jnp.where(lower_half, pltpu.roll(block[0:32], 64, 1), block[32:64])
     block = raw[0:64, 0:128]
     a_send[1] = jnp.where(lower_half, block[0:32], pltpu.roll(block[32:64], 64, 1))
+    for half in range(2):
+        columns = slice(half * LANES, (half + 1) * LANES)
+        up = pltpu.roll(raw[56:64, columns], 72, 1)
+        down = raw[0:8, columns]
+        for a in range(1, 8):
+            high = raw[a * 64 + 56 : a * 64 + 64, columns]
+            low = raw[a * 64 : a * 64 + 8, columns]
+            up = jnp.where(node == a, pltpu.roll(high, (a * 8 + 72) % 128, 1), up)
+            down = jnp.where(node == a, pltpu.roll(low, a * 8, 1), down)
+        b_send[0, half] = up
+        b_send[1, half] = down
+
+    steps = (1, -1)
 
     def face_copy(i):
-        step = 1 if i % 2 == 0 else -1
         if i < 2:
-            source, sink = a_send.at[i], a_recv.at[i]
-            target = (lax.rem(g + step + grp_count, grp_count), d)
+            source, sink, target = a_send.at[i], a_recv.at[i], wrapped(steps[i], 0)
         else:
-            source, sink = b_send.at[i - 2], b_recv.at[i - 2]
-            target = (g, lax.rem(d + step + dev_count, dev_count))
+            source, sink, target = b_send.at[i - 2], b_recv.at[i - 2], wrapped(0, steps[i - 2])
         return pltpu.make_async_remote_copy(
             src_ref=source, dst_ref=sink,
             send_sem=face_send_sem.at[i], recv_sem=face_recv_sem.at[i],
             device_id=target, device_id_type=MESH,
         )
 
-    def start_faces(first, position, count):
-        @pl.when(position < count - 1)
+    def edge_copy(i, j):
+        return pltpu.make_async_remote_copy(
+            src_ref=b_send.at[j, 1 - i], dst_ref=edge_recv.at[j, i],
+            send_sem=edge_send_sem.at[j, i], recv_sem=edge_recv_sem.at[j, i],
+            device_id=wrapped(steps[i], steps[j]), device_id_type=MESH,
+        )
+
+    sends_a, sends_b = (g < grp_count - 1, g > 0), (d < dev_count - 1, d > 0)
+    gets_a, gets_b = (g > 0, g < grp_count - 1), (d > 0, d < dev_count - 1)
+
+    def when(condition, action):
+        @pl.when(condition)
         def _():
-            face_copy(first).start()
-
-        @pl.when(position > 0)
-        def _():
-            face_copy(first + 1).start()
-
-    def finish_faces(first, position, count, sink):
-        @pl.when(position > 0)
-        def _():
-            face_copy(first).wait_recv()
-
-        @pl.when(position == 0)
-        def _():
-            sink[0] = jnp.zeros_like(sink[0])
-
-        @pl.when(position < count - 1)
-        def _():
-            face_copy(first + 1).wait_recv()
-
-        @pl.when(position == count - 1)
-        def _():
-            sink[1] = jnp.zeros_like(sink[1])
-
-    start_faces(0, g, grp_count)
-    finish_faces(0, g, grp_count, a_recv)
+            action()
+
+    def clear(ref, i):
+        ref[i] = jnp.zeros_like(ref[i])
+
+    for j in range(2):
+        for i in range(2):
+            when(sends_a[i] & sends_b[j], lambda: edge_copy(i, j).start())
+    for i in range(2):
+        when(sends_a[i], lambda: face_copy(i).start())
+        when(sends_b[i], lambda: face_copy(2 + i).start())
+
+    for i in range(2):
+        when(gets_a[i], lambda: face_copy(i).wait_recv())
+        when(jnp.logical_not(gets_a[i]), lambda: clear(a_recv, i))
     low, high = raw[0:64, :], raw[448:512, :]
     from_low, from_high = a_recv[0], a_recv[1]
     from_low = jnp.concatenate([from_low, pltpu.roll(from_low, 64, 1)], axis=0)
@@ -259,34 +298,35 @@
     raw[448:512, 0:128] = high[:, :128] + jnp.where(lower_half, low_rolled[0], low_rolled[1])
     raw[448:512, 128:256] = high[:, 128:] + jnp.where(lower_half, low_rolled[1], from_high)
 
-    ey = (lane // 8) % 8
+    faces = []
+    for j in range(2):
+        when(gets_b[j], lambda: face_copy(2 + j).wait_recv())
+        when(jnp.logical_not(gets_b[j]), lambda: clear(b_recv, j))
+        for i in range(2):
+            both = gets_a[i] & gets_b[j]
+            when(both, lambda: edge_copy(i, j).wait_recv())
+            when(jnp.logical_not(both), lambda: clear(edge_recv, (j, i)))
+        first, second = b_recv[j, 0], b_recv[j, 1]
+        up = [pltpu.roll(x, 8, 1) for x in (edge_recv[j, 0], first, second)]
+        down = [pltpu.roll(x, 120, 1) for x in (first, second, edge_recv[j, 1])]
+        face = []
+        for half, own in enumerate((first, second)):
+            from_low = jnp.where(lower_half, up[half], up[half + 1])
+            from_high = jnp.where(lower_half, down[half], down[half + 1])
+            face.append(
+                own + jnp.where(node == 0, from_low, jnp.where(node == 7, from_high, 0.0))
+            )
+        faces.append(face)
     for half in range(2):
         columns = slice(half * LANES, (half + 1) * LANES)
-        up = raw[56:64, columns]
-        up = pltpu.roll(up, 72, 1)
-        down = raw[0:8, columns]
-        for a in range(1, 8):
-            up = jnp.where(
-                ey == a, pltpu.roll(raw[a * 64 + 56 : a * 64 + 64, columns], (a * 8 + 72) % 128, 1), up
-            )
-            down = jnp.where(
-                ey == a, pltpu.roll(raw[a * 64 : a * 64 + 8, columns], a * 8, 1), down
-            )
-        b_send[0, half] = up
-        b_send[1, half] = down
-    start_faces(2, d, dev_count)
-    finish_faces(2, d, dev_count, b_recv)
-    for half in range(2):
-        columns = slice(half * LANES, (half + 1) * LANES)
-        from_low, from_high = b_recv[0, half], b_recv[1, half]
         for a in range(8):
             low_rows = slice(a * 64, a * 64 + 8)
             high_rows = slice(a * 64 + 56, a * 64 + 64)
             low, high = raw[low_rows, columns], raw[high_rows, columns]
-            got_low = pltpu.roll(from_low, (128 - a * 8) % 128, 1)
-            got_high = pltpu.roll(from_high, (56 - a * 8) % 128, 1)
-            raw[low_rows, columns] = low + jnp.where(ey == 0, got_low, pltpu.roll(high, 8, 1))
-            raw[high_rows, columns] = high + jnp.where(ey == 7, got_high, pltpu.roll(low, 120, 1))
+            got_low = pltpu.roll(faces[0][half], (128 - a * 8) % 128, 1)
+            got_high = pltpu.roll(faces[1][half], (56 - a * 8) % 128, 1)
+            raw[low_rows, columns] = low + jnp.where(node == 0, got_low, pltpu.roll(high, 8, 1))
+            raw[high_rows, columns] = high + jnp.where(node == 7, got_high, pltpu.roll(low, 120, 1))
 
     ez = lax.broadcasted_iota(jnp.int32, (1, 8, LANES), 2) % 8
     c = lax.broadcasted_iota(jnp.int32, (1, 8, LANES), 1)
@@ -312,14 +352,11 @@
         cost_copy(j).wait_send()
     for j in range(1, grp_count):
         group_copy(j).wait_send()
-    for first, position, count in ((0, g, grp_count), (2, d, dev_count)):
-        @pl.when(position < count - 1)
-        def _():
-            face_copy(first).wait_send()
-
-        @pl.when(position > 0)
-        def _():
-            face_copy(first + 1).wait_send()
+    for i in range(2):
+        when(sends_a[i], lambda: face_copy(i).wait_send())
+        when(sends_b[i], lambda: face_copy(2 + i).wait_send())
+        for j in range(2):
+            when(sends_a[i] & sends_b[j], lambda: edge_copy(i, j).wait_send())
 
 
 def on_device(obs_coord, obs_resid, obs_weight, obs_dest, obs_send_slot, obs_elem, obs_slot):
@@ -334,12 +371,18 @@
     field, cost = pl.pallas_call(
         functools.partial(kernel, dev_count, grp_count, capacity),
         out_shape=(
-            jax.ShapeDtypeStruct((ELEM_DEV, 512), F32),
-            jax.ShapeDtypeStruct((1, LANES), F32),
+            pltpu.VMEM((ELEM_DEV, 512), F32),
+            pltpu.VMEM((1, LANES), F32),
         ),
-        in_specs=[vmem] * 6,
+        in_specs=[pl.BlockSpec(memory_space=pl.ANY)] * 6,
         out_specs=(vmem, vmem),
         scratch_shapes=[
+            pltpu.VMEM((3, row_count), F32),
+            pltpu.VMEM((1, row_count), F32),
+            pltpu.VMEM((1, row_count), F32),
+            pltpu.VMEM((1, row_count), jnp.int32),
+            pltpu.VMEM((1, row_count), jnp.int32),
+            pltpu.VMEM((1, row_count), jnp.int32),
             pltpu.VMEM((5 * 2 * row_count // LANES, LANES), F32),
             pltpu.VMEM((dev_count, 5 * per_dest, LANES), F32),
             pltpu.VMEM((dev_count, 5 * per_dest, LANES), F32),
@@ -365,6 +408,10 @@
             dma((grp_count,)),
             dma((4,)),
             dma((4,)),
+            pltpu.VMEM((2, 2, 8, LANES), F32),
+            dma((2, 2)),
+            dma((2, 2)),
+            dma((6,)),
         ],
         compiler_params=pltpu.CompilerParams(collective_id=0, has_side_effects=True),
     )(obs_coord, *rows)

time: 26.9 us -> 22.7 us (0.84)
  the two profiles are of different devices: /device:TPU:1 before, /device:TPU:0 now
where the time goes in v2:
time: 22.7 us; the launch traced here: 22.4 us
  Pallas kernels  19.8 us (87%)
  between operations  1.8 us (8%)
  local copies, waits for them, and re-layouts  0.8 us (4%)
    pallas_call x1, Pallas kernels, on_device(): pl.pallas_call(functools.partial(kernel, dev_count, grp_count, capacity),...  19.8 us
    unnamed x1, local copies, waits for them, and re-layouts  0.8 us

profile of v2, /device:TPU:0, one launch (start us, length us, event | category | flops | bytes accessed | tf_op | source)
XLA Modules:
  0.0 22.4 jit_solution(18337581437548935785)
XLA Ops:
  0.6 19.8 %shard_map.77 = (f32[256,512]{1,0:T(8,128)S(1)}, f32[1,128]{1,0:T(1,128)S(1)}) custom-call(f32[3,4096]{1,0:T(4,128)} %coord_in.1, f32[1,4096]{1,0:T(1,128)} %bitcast.10, f32[1,4096]{1,0:T(1,128)} %bitcast.11, s32[1,4096]{1,0:T(1,128)} %bitcast.12, s32[1,4096]{1,0:T(1,128)} %bitcast.13, s32[1,4096]{1,0:T(1,128)} %bitcast.14), custom_call_target="tpu_custom_call" | custom-call | tf_op jit(solution)/shard_map/pallas_call | solution.py:371
  20.4 0.8 %copy.10 = f32[4,8,8,512]{3,2,1,0:T(8,128)} copy(f32[4,8,8,512]{3,2,1,0:T(8,128)S(1)} %bitcast.8) | data formatting | bytes 1048576

commit v3 on v2

--- a/solution.py
+++ b/solution.py
@@ -19,6 +19,10 @@
 BF16 = jnp.bfloat16
 
 ANCHORS = [-math.cos(math.pi * k / 7) for k in range(8)]
+OUTER_PAIRS = [(a, b) for a in (0, 7) for b in range(8)]
+OUTER_PAIRS += [(a, b) for a in range(1, 7) for b in (0, 7)]
+INNER_PAIRS = [(a, b) for a in range(1, 7) for b in range(1, 7)]
+PAIRS = OUTER_PAIRS + INNER_PAIRS
 COEFS = [
     1.0 / math.prod(ANCHORS[a] - ANCHORS[m] for m in range(8) if m != a) for a in range(8)
 ]
@@ -63,6 +67,7 @@
     third, outer, p_high, p_low, onehot, raw, a_send, a_recv, b_send, b_recv,
     send_sem, recv_sem, cost_send_sem, cost_recv_sem, group_send_sem, group_recv_sem,
     face_send_sem, face_recv_sem, edge_recv, edge_send_sem, edge_recv_sem, load_sem,
+    face_rows, inner_rows,
 ):
     g = lax.axis_index("grp")
     d = lax.axis_index("dev")
@@ -175,7 +180,21 @@
         data_copy(j).start()
     recv[0] = send[d]
 
-    raw[...] = jnp.zeros_like(raw)
+    face_rows[...] = jnp.zeros_like(face_rows)
+    inner_rows[...] = jnp.zeros_like(inner_rows)
+
+    def products(k, h, pairs):
+        count = pairs.stop - pairs.start
+        lanes = slice(h * LANES, (h + 1) * LANES)
+        product = outer[k, pairs, h : h + 1, :] * third[k, :, h, :][None]
+        product = product.reshape(count * 8, LANES)
+        rounded = product.astype(BF16)
+        p_high[0 : count * 8, lanes] = rounded
+        p_low[0 : count * 8, lanes] = (product - rounded.astype(F32)).astype(BF16)
+
+    def add_sums(k, sums):
+        rows = slice(0, sums.shape[0])
+        sums[...] += dot_nt(p_high[rows], onehot[k]) + dot_nt(p_low[rows], onehot[k])
 
     def element_sums(k, carry):
         for i in range(per_chunk):
@@ -195,22 +214,18 @@
         third_w = basis_values(channel(2))
         forcing = channel(3)
         owner = channel(4).astype(jnp.int32)
-        for a in range(8):
-            weighted = first_w[a] * forcing
-            third[a] = third_w[a]
-            for b in range(8):
-                outer[a * 8 + b] = weighted * second_w[b]
+        weighted = [first * forcing for first in first_w]
+        for c in range(8):
+            third[k, c] = third_w[c]
+        for i, (a, b) in enumerate(PAIRS):
+            outer[k, i] = weighted[a] * second_w[b]
         ids = lax.broadcasted_iota(jnp.int32, (ELEM_DEV, LANES), 0)
         for h in range(8):
-            lanes = slice(h * LANES, (h + 1) * LANES)
-            product = (outer[:, h : h + 1, :] * third[:, h, :][None]).reshape(512, LANES)
-            rounded = product.astype(BF16)
-            p_high[:, lanes] = rounded
-            p_low[:, lanes] = (product - rounded.astype(F32)).astype(BF16)
-            onehot[:, lanes] = jnp.where(
+            products(k, h, slice(0, len(OUTER_PAIRS)))
+            onehot[k, :, h * LANES : (h + 1) * LANES] = jnp.where(
                 ids == jnp.broadcast_to(owner[h : h + 1, :], (ELEM_DEV, LANES)), 1.0, 0.0
             ).astype(BF16)
-        raw[...] += dot_nt(p_high[...], onehot[...]) + dot_nt(p_low[...], onehot[...])
+        add_sums(k, face_rows)
         return carry
 
     chunk_count = dev_count // per_chunk
@@ -226,6 +241,13 @@
         group_copy(j).start()
 
     lax.fori_loop(middle, chunk_count, element_sums, 0)
+
+    def place(sums, pairs):
+        for i, (a, b) in enumerate(pairs):
+            start = a * 64 + b * 8
+            raw[start : start + 8, :] = sums[i * 8 : i * 8 + 8, :]
+
+    place(face_rows, OUTER_PAIRS)
 
     lane = lax.broadcasted_iota(jnp.int32, (1, LANES), 1)
     lower_half = lane < 64
@@ -283,6 +305,15 @@
     for i in range(2):
         when(sends_a[i], lambda: face_copy(i).start())
         when(sends_b[i], lambda: face_copy(2 + i).start())
+
+    def inner_sums(k, carry):
+        for h in range(8):
+            products(k, h, slice(len(OUTER_PAIRS), len(PAIRS)))
+        add_sums(k, inner_rows)
+        return carry
+
+    lax.fori_loop(0, chunk_count, inner_sums, 0)
+    place(inner_rows, INNER_PAIRS)
 
     for i in range(2):
         when(gets_a[i], lambda: face_copy(i).wait_recv())
@@ -365,6 +396,7 @@
     row_count = obs_resid.shape[0]
     capacity = 2 * row_count // dev_count
     per_dest = capacity // LANES
+    chunks = 2 * row_count // CHUNK
     vmem = pl.BlockSpec(memory_space=pltpu.VMEM)
     dma = pltpu.SemaphoreType.DMA
     rows = [x.reshape(1, row_count) for x in (obs_resid, obs_weight, obs_dest, obs_send_slot, obs_elem)]
@@ -390,11 +422,11 @@
             pltpu.VMEM((dev_count, 1, LANES), F32),
             pltpu.VMEM((1, LANES), F32),
             pltpu.VMEM((grp_count, 1, LANES), F32),
-            pltpu.VMEM((8, 8, LANES), F32),
-            pltpu.VMEM((64, 8, LANES), F32),
-            pltpu.VMEM((512, CHUNK), BF16),
-            pltpu.VMEM((512, CHUNK), BF16),
-            pltpu.VMEM((ELEM_DEV, CHUNK), BF16),
+            pltpu.VMEM((chunks, 8, 8, LANES), F32),
+            pltpu.VMEM((chunks, 64, 8, LANES), F32),
+            pltpu.VMEM((len(INNER_PAIRS) * 8, CHUNK), BF16),
+            pltpu.VMEM((len(INNER_PAIRS) * 8, CHUNK), BF16),
+            pltpu.VMEM((chunks, ELEM_DEV, CHUNK), BF16),
             pltpu.VMEM((512, ELEM_DEV), F32),
             pltpu.VMEM((2, 32, LANES), F32),
             pltpu.VMEM((2, 32, LANES), F32),
@@ -412,6 +444,8 @@
             dma((2, 2)),
             dma((2, 2)),
             dma((6,)),
+            pltpu.VMEM((len(OUTER_PAIRS) * 8, ELEM_DEV), F32),
+            pltpu.VMEM((len(INNER_PAIRS) * 8, ELEM_DEV), F32),
         ],
         compiler_params=pltpu.CompilerParams(collective_id=0, has_side_effects=True),
     )(obs_coord, *rows)

time: 22.7 us -> 22.2 us (0.978)
  Pallas kernels: 19.8 us -> 19.3 us
    pallas_call x1, Pallas kernels: 19.8 us -> 19.3 us  [on_device(): pl.pallas_call(functools.partial(kernel, dev_count, grp_count, capacity),...]
where the time goes in v3:
time: 22.2 us; the launch traced here: 21.9 us
  Pallas kernels  19.3 us (87%)
  between operations  1.8 us (8%)
  local copies, waits for them, and re-layouts  0.8 us (4%)
    pallas_call x1, Pallas kernels, on_device(): pl.pallas_call(functools.partial(kernel, dev_count, grp_count, capacity),...  19.3 us
    unnamed x1, local copies, waits for them, and re-layouts  0.8 us

profile of v3, /device:TPU:0, one launch (start us, length us, event | category | flops | bytes accessed | tf_op | source)
XLA Modules:
  0.0 21.9 jit_solution(3202386924554281859)
XLA Ops:
  0.6 19.3 %shard_map.77 = (f32[256,512]{1,0:T(8,128)S(1)}, f32[1,128]{1,0:T(1,128)S(1)}) custom-call(f32[3,4096]{1,0:T(4,128)} %coord_in.1, f32[1,4096]{1,0:T(1,128)} %bitcast.10, f32[1,4096]{1,0:T(1,128)} %bitcast.11, s32[1,4096]{1,0:T(1,128)} %bitcast.12, s32[1,4096]{1,0:T(1,128)} %bitcast.13, s32[1,4096]{1,0:T(1,128)} %bitcast.14), custom_call_target="tpu_custom_call" | custom-call | tf_op jit(solution)/shard_map/pallas_call | solution.py:403
  20.0 0.8 %copy.10 = f32[4,8,8,512]{3,2,1,0:T(8,128)} copy(f32[4,8,8,512]{3,2,1,0:T(8,128)S(1)} %bitcast.8) | data formatting | bytes 1048576

commit v4 on v3

--- a/solution.py
+++ b/solution.py
@@ -142,7 +142,7 @@
             acc[0 : left.shape[0], :] += dot_nt(left, lane_hot)
         return total + forcing * residual
 
-    total = lax.fori_loop(0, row_count // CHUNK, pack, jnp.zeros((1, CHUNK), F32))
+    total = lax.fori_loop(0, row_count // CHUNK, pack, jnp.zeros((1, CHUNK), F32), unroll=True)
     part = jnp.broadcast_to(0.5 * jnp.sum(total, axis=1, keepdims=True), (1, LANES))
     cost_send[...] = part
     for p in range(dev_count):
@@ -229,18 +229,7 @@
         return carry
 
     chunk_count = dev_count // per_chunk
-    middle = chunk_count // 2
-    lax.fori_loop(0, middle, element_sums, 0)
-
-    group_cost = cost_send[...]
-    for j in range(1, dev_count):
-        cost_copy(j).wait_recv()
-        group_cost = group_cost + cost_recv[j]
-    group_send[...] = group_cost
-    for j in range(1, grp_count):
-        group_copy(j).start()
-
-    lax.fori_loop(middle, chunk_count, element_sums, 0)
+    lax.fori_loop(0, chunk_count, element_sums, 0)
 
     def place(sums, pairs):
         for i, (a, b) in enumerate(pairs):
@@ -305,6 +294,14 @@
     for i in range(2):
         when(sends_a[i], lambda: face_copy(i).start())
         when(sends_b[i], lambda: face_copy(2 + i).start())
+
+    group_cost = cost_send[...]
+    for j in range(1, dev_count):
+        cost_copy(j).wait_recv()
+        group_cost = group_cost + cost_recv[j]
+    group_send[...] = group_cost
+    for j in range(1, grp_count):
+        group_copy(j).start()
 
     def inner_sums(k, carry):
         for h in range(8):

time: 22.2 us -> 21.6 us (0.973)
  Pallas kernels: 19.3 us -> 18.7 us
    pallas_call x1, Pallas kernels: 19.3 us -> 18.7 us  [on_device(): pl.pallas_call(functools.partial(kernel, dev_count, grp_count, capacity),...]
where the time goes in v4:
time: 21.6 us; the launch traced here: 21.3 us
  Pallas kernels  18.7 us (87%)
  between operations  1.8 us (8%)
  local copies, waits for them, and re-layouts  0.8 us (4%)
    pallas_call x1, Pallas kernels, on_device(): pl.pallas_call(functools.partial(kernel, dev_count, grp_count, capacity),...  18.7 us
    unnamed x1, local copies, waits for them, and re-layouts  0.8 us

profile of v4, /device:TPU:0, one launch (start us, length us, event | category | flops | bytes accessed | tf_op | source)
XLA Modules:
  0.0 21.3 jit_solution(4982916550540519658)
XLA Ops:
  0.6 18.7 %shard_map.77 = (f32[256,512]{1,0:T(8,128)S(1)}, f32[1,128]{1,0:T(1,128)S(1)}) custom-call(f32[3,4096]{1,0:T(4,128)} %coord_in.1, f32[1,4096]{1,0:T(1,128)} %bitcast.10, f32[1,4096]{1,0:T(1,128)} %bitcast.11, s32[1,4096]{1,0:T(1,128)} %bitcast.12, s32[1,4096]{1,0:T(1,128)} %bitcast.13, s32[1,4096]{1,0:T(1,128)} %bitcast.14), custom_call_target="tpu_custom_call" | custom-call | tf_op jit(solution)/shard_map/pallas_call | solution.py:400
  19.4 0.8 %copy.10 = f32[4,8,8,512]{3,2,1,0:T(8,128)} copy(f32[4,8,8,512]{3,2,1,0:T(8,128)S(1)} %bitcast.8) | data formatting | bytes 1048576
